TPU v7x, 128 devices: a whole 4x4x4 slice. The times are simulated.
128 devices in a mesh: fsdp: 32 (over x_hi, z, y), tensor: 4 (over x_lo, core).
Axes of the slice: x: 4 (x_hi: 2, x_lo: 2; x = x_hi * 2 + x_lo), y: 4, z: 4, core: 2. Of those that a mesh axis runs over, the one named last changes fastest.
Arguments:
- activations: bfloat16 [32768, 5120], P('fsdp', 'tensor'), may hold values from -6 to 6
- cotangent: bfloat16 [32768, 5120], P('fsdp', 'tensor'), may hold values from -0.032958984 to 0.032958984
- weights: float32 [5120, 5120], P(None, ('tensor', 'fsdp')), may hold values from -0.025 to 0.025
- first_moment: float32 [5120, 5120], P(None, ('tensor', 'fsdp')), may hold values from -3 to 3
- second_moment: float32 [5120, 5120], P(None, ('tensor', 'fsdp')), may hold values from 0.01 to 1
Outputs:
- weights_new: float32 [5120, 5120], P('fsdp', 'tensor')
- first_new: float32 [5120, 5120], P('fsdp', 'tensor')
- second_new: float32 [5120, 5120], P('fsdp', 'tensor')
- weights_bf16: bfloat16 [5120, 5120], P(None, 'tensor')
All inputs are finite; a program needn't handle non-finite values.
Results may differ from a plain program's by a relative error of at most 0.014.
Values may be sent and summed in bfloat16 or wider, within the bound.
No kernel may reach another device: no remote copies, remote signals or barrier semaphores. Data moves between devices by JAX's collectives and lax.ppermute only.
A program may use at most 128 MiB of HBM per device.

v0:
```python
import jax
import jax.numpy as jnp
from jax import lax
from jax.sharding import PartitionSpec as P

STEP = 20
beta_one = 0.9
beta_two = 0.95
adam_eps = 1e-08
learn_rate = 0.0003
decay_rate = 0.1


def split_up(value, dim, count):
    before, after = (value.shape[:dim], value.shape[dim + 1 :])
    return jnp.moveaxis(value.reshape(*before, count, -1, *after), dim, 0)


def sent_and_summed(value, axis, dim):
    count = lax.axis_size(axis)
    parts = lax.all_to_all(split_up(value, dim, count), axis, 0, 0, tiled=True)
    return jnp.sum(parts.astype(jnp.float32), axis=0)


def adam_update(weights, first_moment, second_moment, gradient):
    first_new = beta_one * first_moment + (1.0 - beta_one) * gradient
    second_new = beta_two * second_moment + (1.0 - beta_two) * gradient * gradient
    corrected = first_new / (1.0 - beta_one**STEP)
    scaled = jnp.sqrt(second_new / (1.0 - beta_two**STEP)) + adam_eps
    weights_new = weights - learn_rate * (corrected / scaled + decay_rate * weights)
    return (weights_new, first_new, second_new)


def body(activations, cotangent, weights, first_moment, second_moment):
    gathered = lax.all_gather(activations, "tensor", axis=1, tiled=True)
    transposed = sent_and_summed(
        lax.dot_general(
            cotangent, gathered, (((0,), (0,)), ((), ())), preferred_element_type=jnp.float32
        ).astype(jnp.bfloat16),
        "fsdp",
        0,
    )
    gradient = transposed.T
    weights_old, first_old, second_old = adam_update(weights, first_moment, second_moment, gradient)
    weights_bf16 = lax.all_gather(weights_old.astype(jnp.bfloat16), "fsdp", axis=1, tiled=True)
    weights_new, first_new, second_new = (
        lax.all_to_all(
            weights_old.astype(jnp.bfloat16), "fsdp", split_axis=0, concat_axis=1, tiled=True
        ).astype(weights_old.dtype),
        lax.all_to_all(
            first_old.astype(jnp.bfloat16), "fsdp", split_axis=0, concat_axis=1, tiled=True
        ).astype(first_old.dtype),
        lax.all_to_all(
            second_old.astype(jnp.bfloat16), "fsdp", split_axis=0, concat_axis=1, tiled=True
        ).astype(second_old.dtype),
    )
    return (weights_new, first_new, second_new, weights_bf16)


def solution(mesh):
    return jax.shard_map(
        body,
        mesh=mesh,
        in_specs=(
            P("fsdp", "tensor"),
            P("fsdp", "tensor"),
            P(None, ("tensor", "fsdp")),
            P(None, ("tensor", "fsdp")),
            P(None, ("tensor", "fsdp")),
        ),
        out_specs=(
            P("fsdp", "tensor"),
            P("fsdp", "tensor"),
            P("fsdp", "tensor"),
            P(None, "tensor"),
        ),
        check_vma=False,
    )
```

profile of v0, /device:TPU:0, one launch (start us, length us, event | category | flops | bytes accessed | tf_op | source)
XLA Modules:
  0.0 469.7 jit_solution(9544911949169199346)
XLA Ops:
  7.2 0.0 copy-start
  7.2 0.0 all-gather.3.cloned.1.call-start
  7.2 0.7 all-gather.3.cloned.1.call-update
  7.9 0.0 all-gather.5.cloned.1.call-start
  8.0 101.3 %all-gather.3.cloned.1.call-done = bf16[1024,5120]{1,0:T(8,128)(2,1)} async-done(((bf16[1024,1280]{1,0:T(8,128)(2,1)}), bf16[1024,5120]{1,0:T(8,128)(2,1)}) %all-gather.3.cloned.1.call-update) | async-done | bytes 10485776 | tf_op jit(solution)/shard_map/all_gather | solution.py:35
  109.3 20.2 %convolution_convert_fusion = bf16[1280,5120]{1,0:T(8,128)(2,1)} fusion(bf16[1024,1280]{1,0:T(8,128)(2,1)S(1)} %copy-done, bf16[1024,5120]{1,0:T(8,128)(2,1)} %all-gather.3.cloned.1.call-done), kind=kOutput, calls=%fused_computation.1 | convolution fusion | flops 13428326400 | bytes 26214400 | tf_op jit(solution)/shard_map/dot_general | solution.py:37
  129.5 158.0 %all_to_all.44 = bf16[32,40,5120]{2,1,0:T(8,128)(2,1)} all-to-all(bf16[32,40,5120]{2,1,0:T(8,128)(2,1)} %bitcast.31), channel_id=1, replica_groups=mesh['fsdp'=32,'tensor'=4] {'fsdp'}, dimensions={0} | all-to-all | bytes 26214400 | tf_op jit(solution)/shard_map/all_to_all | solution.py:21
  287.4 7.7 %convert_reduce_fusion = f32[40,5120]{1,0:T(8,128)S(1)} fusion(bf16[32,40,5120]{2,1,0:T(8,128)(2,1)} %all_to_all.44), kind=kLoop, calls=%fused_computation | loop fusion | flops 12902400 | bytes 13926400 | tf_op jit(solution)/shard_map/reduce_sum | solution.py:22
  295.1 0.0 copy-done.2
  295.1 0.0 copy-done.3
  295.1 2.6 fusion.3
  297.7 0.0 all-gather.5.cloned.1.call-update
  297.7 0.8 all_to_all.38
  298.5 1.2 copy.28
  299.7 7.0 %all-to-all-start.3 = ((bf16[32,160,40]{1,2,0:T(8,128)(2,1)}), bf16[32,160,40]{1,2,0:T(8,128)(2,1)S(1)}, u32[]{:S(2)}, u32[]{:S(2)}) async-start(bf16[32,160,40]{1,2,0:T(8,128)(2,1)} %copy.28), calls=%async_computation.3 | async-start | bytes 1310720 | tf_op jit(solution)/shard_map/all_to_all | solution.py:53
  306.8 0.8 all_to_all.36
  307.6 1.2 copy.27
  308.8 13.6 %all-to-all-done.3 = bf16[32,160,40]{1,2,0:T(8,128)(2,1)S(1)} async-done(((bf16[32,160,40]{1,2,0:T(8,128)(2,1)}), bf16[32,160,40]{1,2,0:T(8,128)(2,1)S(1)}, u32[]{:S(2)}, u32[]{:S(2)}) %all-to-all-start.3) | async-done | bytes 409632 | tf_op jit(solution)/shard_map/all_to_all | solution.py:53
  322.4 4.7 %all-to-all-start.2 = ((bf16[32,160,40]{1,2,0:T(8,128)(2,1)}), bf16[32,160,40]{1,2,0:T(8,128)(2,1)S(1)}, u32[]{:S(2)}, u32[]{:S(2)}) async-start(bf16[32,160,40]{1,2,0:T(8,128)(2,1)} %copy.27), calls=%async_computation.2 | async-start | bytes 1310720 | tf_op jit(solution)/shard_map/all_to_all | solution.py:50
  327.1 1.8 all_to_all.34
  328.9 1.2 copy.26
  330.1 10.4 %all-to-all-done.2 = bf16[32,160,40]{1,2,0:T(8,128)(2,1)S(1)} async-done(((bf16[32,160,40]{1,2,0:T(8,128)(2,1)}), bf16[32,160,40]{1,2,0:T(8,128)(2,1)S(1)}, u32[]{:S(2)}, u32[]{:S(2)}) %all-to-all-start.2) | async-done | bytes 409632 | tf_op jit(solution)/shard_map/all_to_all | solution.py:50
  340.5 4.0 all-to-all-start.1
  344.5 0.1 convert_element_type.62
  344.6 1.3 copy.31
  345.9 0.1 convert_element_type.61
  346.0 1.3 copy.30
  347.2 16.4 %all-to-all-done.1 = bf16[32,160,40]{1,2,0:T(8,128)(2,1)S(1)} async-done(((bf16[32,160,40]{1,2,0:T(8,128)(2,1)}), bf16[32,160,40]{1,2,0:T(8,128)(2,1)S(1)}, u32[]{:S(2)}, u32[]{:S(2)}) %all-to-all-start.1) | async-done | bytes 409632 | tf_op jit(solution)/shard_map/all_to_all | solution.py:47
  363.6 1.2 convert_element_type.60
  364.8 2.7 copy.29
  367.5 77.8 %all-gather.5.cloned.1.call-done = bf16[5120,1280]{0,1:T(8,128)(2,1)} async-done(((bf16[5120,40]{0,1:T(8,128)(2,1)}), bf16[5120,1280]{0,1:T(8,128)(2,1)}) %all-gather.5.cloned.1.call-update) | async-done | bytes 13107216 | tf_op jit(solution)/shard_map/all_gather | solution.py:45
  445.3 17.6 %copy.32 = bf16[5120,1280]{1,0:T(8,128)(2,1)} copy(bf16[5120,1280]{0,1:T(8,128)(2,1)} %all-gather.5.cloned.1.call-done) | data formatting | bytes 26214400
  (5 shorter events, 0.0 us)
Async XLA Ops:
  7.2 102.1 %copy-start = (bf16[1024,1280]{1,0:T(8,128)(2,1)S(1)}, bf16[1024,1280]{1,0:T(8,128)(2,1)}, u32[]{:S(2)}) copy-start(bf16[1024,1280]{1,0:T(8,128)(2,1)} %param.6) | copy-start | bytes 7864324
  7.2 102.1 %all-gather.3.cloned.1.call-start = ((), (), s32[]{:S(2)}) async-start(), calls=%async_computation.4 | async-start | bytes 13107200 | tf_op jit(solution)/shard_map/all_gather | solution.py:35
  7.9 437.4 %all-gather.5.cloned.1.call-start = ((), (), s32[]{:S(2)}) async-start(), calls=%async_computation.5 | async-start | bytes 13516800 | tf_op jit(solution)/shard_map/all_gather | solution.py:45
  287.4 7.7 %copy-start.2 = (f32[5120,40]{0,1:T(8,128)S(1)}, f32[5120,40]{0,1:T(8,128)}, u32[]{:S(2)}) copy-start(f32[5120,40]{0,1:T(8,128)} %param.9) | copy-start | bytes 2457604
  287.4 7.7 %copy-start.3 = (f32[5120,40]{0,1:T(8,128)S(1)}, f32[5120,40]{0,1:T(8,128)}, u32[]{:S(2)}) copy-start(f32[5120,40]{0,1:T(8,128)} %param.7) | copy-start | bytes 2457604
  299.7 22.6 %all-to-all-start.3 = ((bf16[32,160,40]{1,2,0:T(8,128)(2,1)}), bf16[32,160,40]{1,2,0:T(8,128)(2,1)S(1)}, u32[]{:S(2)}, u32[]{:S(2)}) async-start(bf16[32,160,40]{1,2,0:T(8,128)(2,1)} %copy.28), calls=%async_computation.3 | async-start | bytes 1310720 | tf_op jit(solution)/shard_map/all_to_all | solution.py:53
  322.4 18.1 %all-to-all-start.2 = ((bf16[32,160,40]{1,2,0:T(8,128)(2,1)}), bf16[32,160,40]{1,2,0:T(8,128)(2,1)S(1)}, u32[]{:S(2)}, u32[]{:S(2)}) async-start(bf16[32,160,40]{1,2,0:T(8,128)(2,1)} %copy.27), calls=%async_computation.2 | async-start | bytes 1310720 | tf_op jit(solution)/shard_map/all_to_all | solution.py:50
  340.5 23.1 %all-to-all-start.1 = ((bf16[32,160,40]{1,2,0:T(8,128)(2,1)}), bf16[32,160,40]{1,2,0:T(8,128)(2,1)S(1)}, u32[]{:S(2)}, u32[]{:S(2)}) async-start(bf16[32,160,40]{1,2,0:T(8,128)(2,1)} %copy.26), calls=%async_computation.1 | async-start | bytes 1310720 | tf_op jit(solution)/shard_map/all_to_all | solution.py:47
  364.8 98.1 %copy-start.1 = (bf16[1024,1280]{1,0:T(8,128)(2,1)S(1)}, bf16[1024,1280]{1,0:T(8,128)(2,1)}, u32[]{:S(2)}) copy-start(bf16[1024,1280]{1,0:T(8,128)(2,1)} %param.6) | copy-start | bytes 7864324
Sparse Core Ops, SparseCore 0:
  9.6 99.5 all-gather.2
  297.8 147.3 all-gather.4
where the time goes:
time: 471 us; the launch traced here: 470 us
  waiting for transfers between devices  220 us (47%)
  blocking collectives  158 us (34%)
  local copies, waits for them, and re-layouts  29.9 us (6%)
  matrix products  20.2 us (4%)
  starting transfers between devices  15.8 us (3%)
  between operations  14.1 us (3%)
  other arithmetic  11.6 us (2%)
    all_to_all x1, blocking collectives, sent_and_summed(): parts = lax.all_to_all(split_up(value, dim, count), axis, 0, 0, tiled=True)  158 us
    all_gather x1, waiting for transfers between devices, body(): gathered = lax.all_gather(activations, 'tensor', axis=1, tiled=True)  101 us
    all_gather x1, waiting for transfers between devices, body(): lax.all_gather(weights_old.astype(jnp.bfloat16), 'fsdp', axis=1, tiled=True)  77.8 us
    unnamed x12, local copies, waits for them, and re-layouts  22.9 us
    dot_general x1, matrix products, body(): lax.dot_general(cotangent, gathered, (((0,), (0,)), ((), ())), preferred_...  20.2 us
    all_to_all x1, waiting for transfers between devices, body(): lax.all_to_all(weights_old.astype(jnp.bfloat16), 'fsdp', split_axis=0, co...  16.4 us
    all_to_all x1, waiting for transfers between devices, body(): lax.all_to_all(second_old.astype(jnp.bfloat16), 'fsdp', split_axis=0, con...  13.6 us
    all_to_all x1, waiting for transfers between devices, body(): lax.all_to_all(first_old.astype(jnp.bfloat16), 'fsdp', split_axis=0, conc...  10.4 us
  transfers between devices with their start and end apart: 5, of which 5 were waited for; matrix products, arithmetic and copies ran while one was open for 2% of the time, Pallas kernels for 0%

commit v1 on v0

--- a/solution.py
+++ b/solution.py
@@ -1,3 +1,4 @@
+import functools
 import jax
 import jax.numpy as jnp
 from jax import lax
@@ -9,6 +10,22 @@
 adam_eps = 1e-08
 learn_rate = 0.0003
 decay_rate = 0.1
+
+
+def cycles_create(block_in, mesh_name):
+    carry_in = jnp.concatenate(
+        lax.all_to_all(
+            jnp.stack([block_in for _ in range(lax.axis_size(mesh_name))], 0),
+            split_axis=0,
+            axis_name=mesh_name,
+            concat_axis=0,
+        ),
+        axis=1,
+    )
+    return carry_in
+
+
+move_views = functools.partial(cycles_create, mesh_name="fsdp")
 
 
 def split_up(value, dim, count):
@@ -42,7 +59,7 @@
     )
     gradient = transposed.T
     weights_old, first_old, second_old = adam_update(weights, first_moment, second_moment, gradient)
-    weights_bf16 = lax.all_gather(weights_old.astype(jnp.bfloat16), "fsdp", axis=1, tiled=True)
+    weights_bf16 = move_views(weights_old.astype(jnp.bfloat16))
     weights_new, first_new, second_new = (
         lax.all_to_all(
             weights_old.astype(jnp.bfloat16), "fsdp", split_axis=0, concat_axis=1, tiled=True

time: 471 us -> 603 us (1.28)
  the two profiles are of different devices: /device:TPU:0 before, /device:TPU:98 now
where the time goes in v1:
time: 603 us; the launch traced here: 602 us
  waiting for transfers between devices  323 us (54%)
  blocking collectives  176 us (29%)
  local copies, waits for them, and re-layouts  34.3 us (6%)
  starting transfers between devices  22.4 us (4%)
  matrix products  20.2 us (3%)
  between operations  14.1 us (2%)
  other arithmetic  11.6 us (2%)
    all_to_all x1, waiting for transfers between devices, cycles_create(): lax.all_to_all(jnp.stack([block_in for _ in range(lax.axis_size(mesh_name...  200 us
    all_to_all x1, blocking collectives, sent_and_summed(): parts = lax.all_to_all(split_up(value, dim, count), axis, 0, 0, tiled=True)  158 us
    all_gather x1, waiting for transfers between devices, body(): gathered = lax.all_gather(activations, 'tensor', axis=1, tiled=True)  100 us
    unnamed x12, local copies, waits for them, and re-layouts  21.5 us
    dot_general x1, matrix products, body(): lax.dot_general(cotangent, gathered, (((0,), (0,)), ((), ())), preferred_...  20.2 us
    all_to_all x1, blocking collectives, body(): lax.all_to_all(second_old.astype(jnp.bfloat16), 'fsdp', split_axis=0, con...  17.4 us
  transfers between devices with their start and end apart: 4, of which 4 were waited for; matrix products, arithmetic and copies ran while one was open for 1% of the time, Pallas kernels for 0%

profile of v1, /device:TPU:98, one launch (start us, length us, event | category | flops | bytes accessed | tf_op | source)
XLA Modules:
  0.0 601.8 jit_solution(14103812240310579471)
XLA Ops:
  7.2 0.0 copy-start
  7.2 0.0 all-gather.2.cloned.1.call-start
  7.2 0.7 all-gather.2.cloned.1.call-update
  7.9 100.1 %all-gather.2.cloned.1.call-done = bf16[1024,5120]{1,0:T(8,128)(2,1)} async-done(((bf16[1024,1280]{1,0:T(8,128)(2,1)}), bf16[1024,5120]{1,0:T(8,128)(2,1)}) %all-gather.2.cloned.1.call-update) | async-done | bytes 10485776 | tf_op jit(solution)/shard_map/all_gather | solution.py:52
  108.0 0.0 copy-done
  108.0 20.2 %convolution_convert_fusion = bf16[1280,5120]{1,0:T(8,128)(2,1)} fusion(bf16[1024,1280]{1,0:T(8,128)(2,1)S(1)} %copy-done, bf16[1024,5120]{1,0:T(8,128)(2,1)} %all-gather.2.cloned.1.call-done), kind=kOutput, calls=%fused_computation.1 | convolution fusion | flops 13428326400 | bytes 26214400 | tf_op jit(solution)/shard_map/dot_general | solution.py:54
  128.2 158.4 %all_to_all.49 = bf16[32,40,5120]{2,1,0:T(8,128)(2,1)} all-to-all(bf16[32,40,5120]{2,1,0:T(8,128)(2,1)} %bitcast.34), channel_id=1, replica_groups=mesh['fsdp'=32,'tensor'=4] {'fsdp'}, dimensions={0} | all-to-all | bytes 26214400 | tf_op jit(solution)/shard_map/all_to_all | solution.py:38
  286.7 7.7 %convert_reduce_fusion = f32[40,5120]{1,0:T(8,128)S(1)} fusion(bf16[32,40,5120]{2,1,0:T(8,128)(2,1)} %all_to_all.49), kind=kLoop, calls=%fused_computation | loop fusion | flops 12902400 | bytes 13926400 | tf_op jit(solution)/shard_map/reduce_sum | solution.py:39
  294.3 0.0 copy-done.2
  294.3 0.0 copy-done.3
  294.4 2.5 fusion.3
  296.9 0.8 all_to_all.37
  297.7 1.2 copy.13
  298.9 11.0 %all-to-all-start.1 = ((bf16[32,160,40]{1,2,0:T(8,128)(2,1)}), bf16[32,160,40]{1,2,0:T(8,128)(2,1)S(1)}, u32[]{:S(2)}, u32[]{:S(2)}) async-start(bf16[32,160,40]{1,2,0:T(8,128)(2,1)} %copy.13), calls=%async_computation.1 | async-start | bytes 1310720 | tf_op jit(solution)/shard_map/all_to_all | solution.py:64
  309.9 0.8 all_to_all.39
  310.8 1.2 copy.14
  312.0 11.5 %all-to-all-done.1 = bf16[32,160,40]{1,2,0:T(8,128)(2,1)S(1)} async-done(((bf16[32,160,40]{1,2,0:T(8,128)(2,1)}), bf16[32,160,40]{1,2,0:T(8,128)(2,1)S(1)}, u32[]{:S(2)}, u32[]{:S(2)}) %all-to-all-start.1) | async-done | bytes 409632 | tf_op jit(solution)/shard_map/all_to_all | solution.py:64
  323.5 5.3 all-to-all-start.2
  328.8 1.8 all_to_all.41
  330.6 0.4 copy.15
  331.0 10.8 %all-to-all-done.2 = bf16[32,160,40]{1,2,0:T(8,128)(2,1)S(1)} async-done(((bf16[32,160,40]{1,2,0:T(8,128)(2,1)}), bf16[32,160,40]{1,2,0:T(8,128)(2,1)S(1)}, u32[]{:S(2)}, u32[]{:S(2)}) %all-to-all-start.2) | async-done | bytes 409632 | tf_op jit(solution)/shard_map/all_to_all | solution.py:67
  341.8 17.4 %all_to_all.50 = bf16[32,160,40]{1,2,0:T(8,128)(2,1)} all-to-all(bf16[32,160,40]{1,2,0:T(8,128)(2,1)S(1)} %copy.15), channel_id=1, replica_groups=mesh['fsdp'=32,'tensor'=4] {'fsdp'}, dimensions={0} | all-to-all | bytes 819200 | tf_op jit(solution)/shard_map/all_to_all | solution.py:70
  359.2 6.6 %stack.2 = bf16[32,5120,40]{1,2,0:T(8,128)(2,1)} broadcast(bf16[5120,40]{0,1:T(8,128)(2,1)S(1)} %get-tuple-element.9), dimensions={1,2} | broadcast | bytes 13516800 | tf_op jit(solution)/shard_map/stack | solution.py:18
  365.8 6.1 %all-to-all-start.4 = ((bf16[32,5120,40]{1,2,0:T(8,128)(2,1)}), bf16[32,5120,40]{1,2,0:T(8,128)(2,1)}, u32[]{:S(2)}, u32[]{:S(2)}) async-start(bf16[32,5120,40]{1,2,0:T(8,128)(2,1)} %stack.2), calls=%async_computation.4 | async-start | bytes 26214400 | tf_op jit(solution)/shard_map/all_to_all | solution.py:17
  371.9 0.1 convert_element_type.60
  372.0 1.3 copy.16
  373.3 0.1 convert_element_type.61
  373.4 1.3 copy.17
  374.6 1.2 convert_element_type.62
  375.8 1.3 copy.18
  377.1 200.1 %all-to-all-done.4 = bf16[32,5120,40]{1,2,0:T(8,128)(2,1)} async-done(((bf16[32,5120,40]{1,2,0:T(8,128)(2,1)}), bf16[32,5120,40]{1,2,0:T(8,128)(2,1)}, u32[]{:S(2)}, u32[]{:S(2)}) %all-to-all-start.4) | async-done | bytes 13107232 | tf_op jit(solution)/shard_map/all_to_all | solution.py:17
  577.2 17.7 %copy.19 = bf16[5120,1280]{1,0:T(8,128)(2,1)} copy(bf16[5120,1280]{0,1:T(8,128)(2,1)} %bitcast.9) | data formatting | bytes 26214400
  (4 shorter events, 0.0 us)
Async XLA Ops:
  7.2 100.9 %copy-start = (bf16[1024,1280]{1,0:T(8,128)(2,1)S(1)}, bf16[1024,1280]{1,0:T(8,128)(2,1)}, u32[]{:S(2)}) copy-start(bf16[1024,1280]{1,0:T(8,128)(2,1)} %param.6) | copy-start | bytes 7864324
  7.2 100.9 %all-gather.2.cloned.1.call-start = ((), (), s32[]{:S(2)}) async-start(), calls=%async_computation.5 | async-start | bytes 13107200 | tf_op jit(solution)/shard_map/all_gather | solution.py:52
  286.7 7.7 %copy-start.2 = (f32[5120,40]{0,1:T(8,128)S(1)}, f32[5120,40]{0,1:T(8,128)}, u32[]{:S(2)}) copy-start(f32[5120,40]{0,1:T(8,128)} %param.9) | copy-start | bytes 2457604
  286.7 7.7 %copy-start.3 = (f32[5120,40]{0,1:T(8,128)S(1)}, f32[5120,40]{0,1:T(8,128)}, u32[]{:S(2)}) copy-start(f32[5120,40]{0,1:T(8,128)} %param.7) | copy-start | bytes 2457604
  298.9 24.6 %all-to-all-start.1 = ((bf16[32,160,40]{1,2,0:T(8,128)(2,1)}), bf16[32,160,40]{1,2,0:T(8,128)(2,1)S(1)}, u32[]{:S(2)}, u32[]{:S(2)}) async-start(bf16[32,160,40]{1,2,0:T(8,128)(2,1)} %copy.13), calls=%async_computation.1 | async-start | bytes 1310720 | tf_op jit(solution)/shard_map/all_to_all | solution.py:64
  323.5 18.3 %all-to-all-start.2 = ((bf16[32,160,40]{1,2,0:T(8,128)(2,1)}), bf16[32,160,40]{1,2,0:T(8,128)(2,1)S(1)}, u32[]{:S(2)}, u32[]{:S(2)}) async-start(bf16[32,160,40]{1,2,0:T(8,128)(2,1)} %copy.14), calls=%async_computation.2 | async-start | bytes 1310720 | tf_op jit(solution)/shard_map/all_to_all | solution.py:67
  365.8 211.4 %all-to-all-start.4 = ((bf16[32,5120,40]{1,2,0:T(8,128)(2,1)}), bf16[32,5120,40]{1,2,0:T(8,128)(2,1)}, u32[]{:S(2)}, u32[]{:S(2)}) async-start(bf16[32,5120,40]{1,2,0:T(8,128)(2,1)} %stack.2), calls=%async_computation.4 | async-start | bytes 26214400 | tf_op jit(solution)/shard_map/all_to_all | solution.py:17
  577.2 17.7 %copy-start.1 = (bf16[1024,1280]{1,0:T(8,128)(2,1)S(1)}, bf16[1024,1280]{1,0:T(8,128)(2,1)}, u32[]{:S(2)}) copy-start(bf16[1024,1280]{1,0:T(8,128)(2,1)} %param.6) | copy-start | bytes 7864324
Sparse Core Ops, SparseCore 0:
  9.6 98.3 all-gather.1
